TPU v7x, 32 devices: a whole 2x2x4 slice. The times are simulated.
32 devices in a mesh: section: 4 (over y, x), dp: 8 (over z, core).
Axes of the slice: x: 2, y: 2, z: 4, core: 2. Of those that a mesh axis runs over, the one named last changes fastest.
Arguments:
- descriptors: bfloat16 [4, 4096, 1024], P(None, 'dp'), may hold values from -6 to 6
- layer_weight: bfloat16 [4, 8, 1024, 1024], P('section', None, 'dp'), may hold values from -0.25 to 0.25
- layer_bias: float32 [4, 8, 1024], P('section'), may hold values from -3 to 3
- readout: float32 [8, 1024], replicated, may hold values from -0.75 to 0.75
- self_energy: float32 [8], replicated, may hold values from -2 to -0.5
- tile_species: int32 [4, 32], P(None, 'dp'), may hold values from 0 to 7
- tile_fill: int32 [4, 32], P(None, 'dp'), may hold values from 1 to 128
Outputs:
- atom_energy: float32 [4, 4096], P('section', 'dp')
- energy: float32 [4], replicated
All inputs are finite; a program needn't handle non-finite values.
Results may differ from a plain program's by a relative error of at most 0.0044.
Values may be sent and summed in bfloat16 or wider, within the bound.
No kernel may reach another device: no remote copies, remote signals or barrier semaphores. Data moves between devices by JAX's collectives and lax.ppermute only.
A program may use at most 128 MiB of HBM per device.

v0:
```python
import jax
import jax.numpy as jnp
from jax import lax
from jax.sharding import PartitionSpec as P


def shifted(block, axis, distance):
    devices = range(lax.axis_size(axis))
    route = [(i - distance, i) for i in devices if i - distance in devices]
    return lax.ppermute(block, axis, route)


def smooth_unit(value):
    return jnp.maximum(value, 0.0) + jnp.minimum(jnp.expm1(jnp.minimum(value, 0.0)), 0.0)


def grouped_product(source, weights, species):
    chosen = jnp.take(weights, species, axis=0)
    return jnp.einsum("tai,tio->tao", source, chosen, preferred_element_type=jnp.float32)


def table_rows(onehot, table):
    return jnp.dot(onehot, table, precision=lax.Precision.HIGHEST)


def shards(descriptors, layer_weight, layer_bias, readout, self_energy, tile_species, tile_fill):
    sections = lax.axis_size("section")
    position = lax.axis_index("section")
    batches, atoms_dev, width = descriptors.shape
    tiles_dev = tile_species.shape[1]
    tile = atoms_dev // tiles_dev
    kinds = readout.shape[0]
    atoms_all = atoms_dev * lax.axis_size("dp")
    total_steps = batches + sections - 1
    bias = layer_bias[0]
    is_last = position == sections - 1
    kind_ids = jnp.arange(kinds, dtype=jnp.int32)
    slot_ids = jnp.arange(tile, dtype=jnp.int32)
    incoming = jnp.zeros((atoms_dev, width), jnp.bfloat16)
    stored = jnp.zeros((batches, atoms_dev), jnp.float32)
    energies = jnp.zeros((batches,), jnp.float32)
    weights = None
    for step in range(total_steps):
        batch = step - position
        valid = jnp.logical_and(batch >= 0, batch < batches)
        keep = jnp.logical_and(valid, is_last)
        index = jnp.clip(batch, 0, batches - 1)
        species = lax.dynamic_index_in_dim(tile_species, index, 0, keepdims=False)
        fill = lax.dynamic_index_in_dim(tile_fill, index, 0, keepdims=False)
        first = descriptors[min(step, batches - 1)]
        source = jnp.where(position == 0, first, incoming).reshape(tiles_dev, tile, width)
        if step == 0:
            weights = lax.all_gather(layer_weight[0], "dp", axis=1, tiled=True)
            product = grouped_product(source, weights, species)
        else:
            product = grouped_product(source, weights, species)
        onehot = (species[:, None] == kind_ids[None, :]).astype(jnp.float32)
        active = smooth_unit(product + table_rows(onehot, bias)[:, None, :])
        readout_rows = table_rows(onehot, readout)
        offsets = table_rows(onehot, self_energy[:, None])
        values = jnp.sum(active * readout_rows[:, None, :], axis=-1) + offsets
        present = slot_ids[None, :] < fill[:, None]
        values = jnp.where(jnp.logical_and(present, keep), values, jnp.float32(0.0)).reshape(
            atoms_dev
        )
        stored = stored.at[index].add(values)
        term = jnp.sum(values) / atoms_all
        finished = step - (sections - 1)
        if 0 <= finished < batches:
            energies = energies.at[finished].set(lax.psum(term, ("section", "dp")))
        if step < total_steps - 1:
            incoming = shifted(active.astype(jnp.bfloat16).reshape(atoms_dev, width), "section", 1)
    received = lax.all_to_all(stored, "section", split_axis=0, concat_axis=0, tiled=True)
    mine = received[sections - 1]
    return (mine[None, :], energies)


def solution(mesh):
    placed = (
        P(None, "dp", None),
        P("section", None, "dp", None),
        P("section", None, None),
        P(),
        P(),
        P(None, "dp"),
        P(None, "dp"),
    )
    return jax.shard_map(
        shards, mesh=mesh, in_specs=placed, out_specs=(P("section", "dp"), P()), check_vma=False
    )
```

profile of v0, /device:TPU:12, one launch (start us, length us, event | category | flops | bytes accessed | tf_op | source)
XLA Modules:
  0.0 464.9 jit_solution(16702947367663745943)
XLA Ops:
  12.9 146.2 %all-gather.3.cloned.1.call-done = bf16[1,8,1024,1024]{3,2,1,0:T(8,128)(2,1)} async-done(((bf16[1,8,128,1024]{3,2,1,0:T(8,128)(2,1)}), bf16[1,8,1024,1024]{3,2,1,0:T(8,128)(2,1)}) %all-gather.3.cloned.1.call-update) | async-done | bytes 16777232 | tf_op jit(solution)/shard_map/all_gather | solution.py:53
  159.1 11.7 %fusion.131 = (bf16[8,512,1024]{2,1,0:T(8,128)(2,1)}, bf16[8,512,1024]{2,1,0:T(8,128)(2,1)}) fusion(bf16[8,1024,1024]{2,1,0:T(8,128)(2,1)} %bitcast.146), kind=kLoop, calls=%fused_computation.259 | loop fusion | bytes 33554432 | tf_op jit(solution)/shard_map/jit(_take)/gather | solution.py:18
  170.8 6.2 %gather_fusion = bf16[4,512,1024]{2,1,0:T(8,128)(2,1)} fusion(bf16[8,512,1024]{2,1,0:T(8,128)(2,1)} %get-tuple-element.168, s32[1024]{0:T(1024)S(1)} %pad_clamp_fusion.6), kind=kCustom, calls=%fused_computation.clone | custom fusion | bytes 8388624 | tf_op jit(solution)/shard_map/jit(_take)/gather | solution.py:18
  176.9 6.1 %gather_fusion.1 = bf16[4,512,1024]{2,1,0:T(8,128)(2,1)} fusion(bf16[8,512,1024]{2,1,0:T(8,128)(2,1)} %get-tuple-element.169, s32[1024]{0:T(1024)S(1)} %pad_clamp_fusion.6), kind=kCustom, calls=%fused_computation.1.clone | custom fusion | bytes 8388624 | tf_op jit(solution)/shard_map/jit(_take)/gather | solution.py:18
  193.5 6.2 %gather_fusion.2 = bf16[4,512,1024]{2,1,0:T(8,128)(2,1)} fusion(bf16[8,512,1024]{2,1,0:T(8,128)(2,1)} %get-tuple-element.168, s32[1024]{0:T(1024)S(1)} %pad_clamp_fusion.5), kind=kCustom, calls=%fused_computation.2.clone | custom fusion | bytes 8388624 | tf_op jit(solution)/shard_map/jit(_take)/gather | solution.py:18
  199.7 6.1 %gather_fusion.3 = bf16[4,512,1024]{2,1,0:T(8,128)(2,1)} fusion(bf16[8,512,1024]{2,1,0:T(8,128)(2,1)} %get-tuple-element.169, s32[1024]{0:T(1024)S(1)} %pad_clamp_fusion.5), kind=kCustom, calls=%fused_computation.3.clone | custom fusion | bytes 8388624 | tf_op jit(solution)/shard_map/jit(_take)/gather | solution.py:18
  205.8 10.8 %collective-permute-done = bf16[512,1024]{1,0:T(8,128)(2,1)S(1)} collective-permute-done((bf16[512,1024]{1,0:T(8,128)(2,1)S(1)}, bf16[512,1024]{1,0:T(8,128)(2,1)S(1)}, u32[]{:S(2)}, u32[]{:S(2)}) %collective-permute-start) | collective-permute-done | bytes 1048608 | tf_op jit(solution)/shard_map/ppermute | solution.py:10
  217.9 5.4 %fusion.136 = (bf16[4,128,1024]{2,1,0:T(8,128)(2,1)S(1)}, f32[4,128]{1,0:T(4,128)S(1)}) fusion(f32[4,1024]{1,0:T(4,128)S(1)} %fusion.55, f32[4,1024]{1,0:T(4,128)S(1)} %fusion.45, bf16[4,128,1024]{2,1,0:T(8,128)(2,1)S(1)} %bitcast.148, bf16[4,512,1024]{2,1,0:T(8,128)(2,1)} %gather_fusion.3, bf16[4,512,1024]{2,1,0:T(8,128)(2,1)} %gather_fusion.2, ...), kind=kOutput, calls=%fused_computation.264 | convolution fusion | flops 1098907136 | bytes 10520580 | tf_op jit(solution)/shard_map/tai,tio->tao/dot_general | solution.py:19
  227.0 6.2 %gather_fusion.4 = bf16[4,512,1024]{2,1,0:T(8,128)(2,1)} fusion(bf16[8,512,1024]{2,1,0:T(8,128)(2,1)} %get-tuple-element.168, s32[1024]{0:T(1024)S(1)} %pad_clamp_fusion.4), kind=kCustom, calls=%fused_computation.4.clone | custom fusion | bytes 8388624 | tf_op jit(solution)/shard_map/jit(_take)/gather | solution.py:18
  233.2 6.1 %gather_fusion.5 = bf16[4,512,1024]{2,1,0:T(8,128)(2,1)} fusion(bf16[8,512,1024]{2,1,0:T(8,128)(2,1)} %get-tuple-element.169, s32[1024]{0:T(1024)S(1)} %pad_clamp_fusion.4), kind=kCustom, calls=%fused_computation.5.clone | custom fusion | bytes 8388624 | tf_op jit(solution)/shard_map/jit(_take)/gather | solution.py:18
  239.4 11.2 %collective-permute-done.1 = bf16[512,1024]{1,0:T(8,128)(2,1)S(1)} collective-permute-done((bf16[512,1024]{1,0:T(8,128)(2,1)S(1)}, bf16[512,1024]{1,0:T(8,128)(2,1)S(1)}, u32[]{:S(2)}, u32[]{:S(2)}) %collective-permute-start.1) | collective-permute-done | bytes 1048608 | tf_op jit(solution)/shard_map/ppermute | solution.py:10
  260.3 6.2 %gather_fusion.6 = bf16[4,512,1024]{2,1,0:T(8,128)(2,1)} fusion(bf16[8,512,1024]{2,1,0:T(8,128)(2,1)} %get-tuple-element.168, s32[1024]{0:T(1024)S(1)} %pad_clamp_fusion.3), kind=kCustom, calls=%fused_computation.6.clone | custom fusion | bytes 8388624 | tf_op jit(solution)/shard_map/jit(_take)/gather | solution.py:18
  266.5 6.1 %gather_fusion.7 = bf16[4,512,1024]{2,1,0:T(8,128)(2,1)} fusion(bf16[8,512,1024]{2,1,0:T(8,128)(2,1)} %get-tuple-element.169, s32[1024]{0:T(1024)S(1)} %pad_clamp_fusion.3), kind=kCustom, calls=%fused_computation.7.clone | custom fusion | bytes 8388624 | tf_op jit(solution)/shard_map/jit(_take)/gather | solution.py:18
  272.6 11.2 %collective-permute-done.2 = bf16[512,1024]{1,0:T(8,128)(2,1)S(1)} collective-permute-done((bf16[512,1024]{1,0:T(8,128)(2,1)S(1)}, bf16[512,1024]{1,0:T(8,128)(2,1)S(1)}, u32[]{:S(2)}, u32[]{:S(2)}) %collective-permute-start.2) | collective-permute-done | bytes 1048608 | tf_op jit(solution)/shard_map/ppermute | solution.py:10
  285.1 5.4 %fusion.134 = (bf16[4,128,1024]{2,1,0:T(8,128)(2,1)S(1)}, f32[4,128]{1,0:T(4,128)S(1)}) fusion(f32[4,1024]{1,0:T(4,128)S(1)} %fusion.53, f32[4,1024]{1,0:T(4,128)S(1)} %fusion.41, bf16[4,128,1024]{2,1,0:T(8,128)(2,1)S(1)} %bitcast.150, bf16[4,512,1024]{2,1,0:T(8,128)(2,1)} %gather_fusion.7, bf16[4,512,1024]{2,1,0:T(8,128)(2,1)} %gather_fusion.6, ...), kind=kOutput, calls=%fused_computation.262 | convolution fusion | flops 1098907136 | bytes 10520580 | tf_op jit(solution)/shard_map/tai,tio->tao/dot_general | solution.py:19
  293.5 6.3 %gather_fusion.8 = bf16[4,512,1024]{2,1,0:T(8,128)(2,1)} fusion(bf16[8,512,1024]{2,1,0:T(8,128)(2,1)} %get-tuple-element.168, s32[1024]{0:T(1024)S(1)} %pad_clamp_fusion.2), kind=kCustom, calls=%fused_computation.8.clone | custom fusion | bytes 8388624 | tf_op jit(solution)/shard_map/jit(_take)/gather | solution.py:18
  299.8 6.1 %gather_fusion.9 = bf16[4,512,1024]{2,1,0:T(8,128)(2,1)} fusion(bf16[8,512,1024]{2,1,0:T(8,128)(2,1)} %get-tuple-element.169, s32[1024]{0:T(1024)S(1)} %pad_clamp_fusion.2), kind=kCustom, calls=%fused_computation.9.clone | custom fusion | bytes 8388624 | tf_op jit(solution)/shard_map/jit(_take)/gather | solution.py:18
  305.9 6.2 %gather_fusion.10 = bf16[4,512,1024]{2,1,0:T(8,128)(2,1)} fusion(bf16[8,512,1024]{2,1,0:T(8,128)(2,1)} %get-tuple-element.168, s32[1024]{0:T(1024)S(1)} %pad_clamp_fusion.1), kind=kCustom, calls=%fused_computation.10.clone | custom fusion | bytes 8388624 | tf_op jit(solution)/shard_map/jit(_take)/gather | solution.py:18
  312.1 6.2 %gather_fusion.11 = bf16[4,512,1024]{2,1,0:T(8,128)(2,1)} fusion(bf16[8,512,1024]{2,1,0:T(8,128)(2,1)} %get-tuple-element.169, s32[1024]{0:T(1024)S(1)} %pad_clamp_fusion.1), kind=kCustom, calls=%fused_computation.11.clone | custom fusion | bytes 8388624 | tf_op jit(solution)/shard_map/jit(_take)/gather | solution.py:18
  318.2 6.1 %gather_fusion.12 = bf16[4,512,1024]{2,1,0:T(8,128)(2,1)} fusion(bf16[8,512,1024]{2,1,0:T(8,128)(2,1)} %get-tuple-element.168, s32[1024]{0:T(1024)S(1)} %pad_clamp_fusion), kind=kCustom, calls=%fused_computation.12.clone | custom fusion | bytes 8388624 | tf_op jit(solution)/shard_map/jit(_take)/gather | solution.py:18
  324.4 6.2 %gather_fusion.13 = bf16[4,512,1024]{2,1,0:T(8,128)(2,1)} fusion(bf16[8,512,1024]{2,1,0:T(8,128)(2,1)} %get-tuple-element.169, s32[1024]{0:T(1024)S(1)} %pad_clamp_fusion), kind=kCustom, calls=%fused_computation.13.clone | custom fusion | bytes 8388624 | tf_op jit(solution)/shard_map/jit(_take)/gather | solution.py:18
  342.2 21.4 %collective-permute-done.4 = bf16[512,1024]{1,0:T(8,128)(2,1)S(1)} collective-permute-done((bf16[512,1024]{1,0:T(8,128)(2,1)S(1)}, bf16[512,1024]{1,0:T(8,128)(2,1)S(1)}, u32[]{:S(2)}, u32[]{:S(2)}) %collective-permute-start.4) | collective-permute-done | bytes 1048608 | tf_op jit(solution)/shard_map/ppermute | solution.py:10
  376.3 18.7 %collective-permute-done.5 = bf16[512,1024]{1,0:T(8,128)(2,1)S(1)} collective-permute-done((bf16[512,1024]{1,0:T(8,128)(2,1)S(1)}, bf16[512,1024]{1,0:T(8,128)(2,1)S(1)}, u32[]{:S(2)}, u32[]{:S(2)}) %collective-permute-start.5) | collective-permute-done | bytes 1048608 | tf_op jit(solution)/shard_map/ppermute | solution.py:10
  409.5 45.5 %all-reduce.1 = (f32[1]{0:T(128)}, f32[1]{0:T(128)}, f32[1]{0:T(128)}, f32[1]{0:T(128)}) all-reduce(f32[1]{0:T(128)} %bitcast.62, f32[1]{0:T(128)} %bitcast.63, f32[1]{0:T(128)} %bitcast.64, f32[1]{0:T(128)} %bitcast.65), channel_id=1, replica_groups=mesh['section'=4,'dp'=8] {'section','dp'}, use_global_device_ids=true, to_apply=%region_15.17 | all-reduce | flops 4 | bytes 32 | tf_op jit(solution)/shard_map/psum | solution.py:70
  (97 shorter events, 74.2 us)
Async XLA Ops:
  7.2 3.3 copy-start
  7.2 151.9 %all-gather.3.cloned.1.call-start = ((), (), s32[]{:S(2)}) async-start(), calls=%async_computation.1 | async-start | bytes 18874368 | tf_op jit(solution)/shard_map/all_gather | solution.py:53
  183.1 8.8 %copy-start.2 = (s32[2]{0:T(128)S(1)}, s32[2]{0:T(128)}, u32[]{:S(2)}) copy-start(s32[2]{0:T(128)} %constant.301.clone.1) | copy-start | bytes 28
  183.1 9.6 %copy-start.4 = (f32[8]{0:T(128)S(1)}, f32[8]{0:T(128)}, u32[]{:S(2)}) copy-start(f32[8]{0:T(128)} %param.35) | copy-start | bytes 100
  183.1 10.2 %copy-start.3 = (f32[8,1024]{1,0:T(8,128)S(1)}, f32[8,1024]{1,0:T(8,128)}, u32[]{:S(2)}) copy-start(f32[8,1024]{1,0:T(8,128)} %param.34) | copy-start | bytes 98308
  188.5 28.1 %collective-permute-start = (bf16[512,1024]{1,0:T(8,128)(2,1)S(1)}, bf16[512,1024]{1,0:T(8,128)(2,1)S(1)}, u32[]{:S(2)}, u32[]{:S(2)}) collective-permute-start(bf16[512,1024]{1,0:T(8,128)(2,1)S(1)} %bitcast.164), channel_id=1, source_target_pairs={{0,8},{8,16},{16,24},{1,9},{9,17},{17,25},{2,10},{10,18},{18,26},{... | collective-permute-start | bytes 3145736 | tf_op jit(solution)/shard_map/ppermute | solution.py:10
  223.3 27.3 %collective-permute-start.1 = (bf16[512,1024]{1,0:T(8,128)(2,1)S(1)}, bf16[512,1024]{1,0:T(8,128)(2,1)S(1)}, u32[]{:S(2)}, u32[]{:S(2)}) collective-permute-start(bf16[512,1024]{1,0:T(8,128)(2,1)S(1)} %bitcast.166), channel_id=1, source_target_pairs={{0,8},{8,16},{16,24},{1,9},{9,17},{17,25},{2,10},{10,18},{18,26},{... | collective-permute-start | bytes 3145736 | tf_op jit(solution)/shard_map/ppermute | solution.py:10
  257.4 26.4 %collective-permute-start.2 = (bf16[512,1024]{1,0:T(8,128)(2,1)S(1)}, bf16[512,1024]{1,0:T(8,128)(2,1)S(1)}, u32[]{:S(2)}, u32[]{:S(2)}) collective-permute-start(bf16[512,1024]{1,0:T(8,128)(2,1)S(1)} %bitcast.165), channel_id=1, source_target_pairs={{0,8},{8,16},{16,24},{1,9},{9,17},{17,25},{2,10},{10,18},{18,26},{... | collective-permute-start | bytes 3145736 | tf_op jit(solution)/shard_map/ppermute | solution.py:10
  285.1 7.5 %copy-start.1 = (s32[4,4]{1,0:T(4,128)S(1)}, s32[4,4]{1,0:T(4,128)}, u32[]{:S(2)}) copy-start(s32[4,4]{1,0:T(4,128)} %param.37) | copy-start | bytes 196
  290.5 40.7 %collective-permute-start.3 = (bf16[512,1024]{1,0:T(8,128)(2,1)S(1)}, bf16[512,1024]{1,0:T(8,128)(2,1)S(1)}, u32[]{:S(2)}, u32[]{:S(2)}) collective-permute-start(bf16[512,1024]{1,0:T(8,128)(2,1)S(1)} %bitcast.161), channel_id=1, source_target_pairs={{0,8},{8,16},{16,24},{1,9},{9,17},{17,25},{2,10},{10,18},{18,26},{... | collective-permute-start | bytes 3145736 | tf_op jit(solution)/shard_map/ppermute | solution.py:10
  338.0 25.6 %collective-permute-start.4 = (bf16[512,1024]{1,0:T(8,128)(2,1)S(1)}, bf16[512,1024]{1,0:T(8,128)(2,1)S(1)}, u32[]{:S(2)}, u32[]{:S(2)}) collective-permute-start(bf16[512,1024]{1,0:T(8,128)(2,1)S(1)} %bitcast.163), channel_id=1, source_target_pairs={{0,8},{8,16},{16,24},{1,9},{9,17},{17,25},{2,10},{10,18},{18,26},{... | collective-permute-start | bytes 3145736 | tf_op jit(solution)/shard_map/ppermute | solution.py:10
  370.4 24.7 %collective-permute-start.5 = (bf16[512,1024]{1,0:T(8,128)(2,1)S(1)}, bf16[512,1024]{1,0:T(8,128)(2,1)S(1)}, u32[]{:S(2)}, u32[]{:S(2)}) collective-permute-start(bf16[512,1024]{1,0:T(8,128)(2,1)S(1)} %bitcast.162), channel_id=1, source_target_pairs={{0,8},{8,16},{16,24},{1,9},{9,17},{17,25},{2,10},{10,18},{18,26},{... | collective-permute-start | bytes 3145736 | tf_op jit(solution)/shard_map/ppermute | solution.py:10
  403.7 53.8 %all-to-all-start = ((f32[4,1,512]{2,1,0:T(1,128)}), f32[4,1,512]{2,1,0:T(1,128)S(1)}, u32[]{:S(2)}, u32[]{:S(2)}) async-start(f32[4,1,512]{2,1,0:T(1,128)} %constant_dynamic-update-slice_fusion), calls=%async_computation | async-start | bytes 16384 | tf_op jit(solution)/shard_map/all_to_all | solution.py:73
  457.4 0.6 copy-start.5
Sparse Core Ops, SparseCore 0:
  9.6 149.4 all-gather.2
where the time goes:
time: 466 us; the launch traced here: 465 us
  waiting for transfers between devices  220 us (47%)
  local copies, waits for them, and re-layouts  102 us (22%)
  blocking collectives  45.5 us (10%)
  matrix products  42.8 us (9%)
  other arithmetic  20.5 us (4%)
  starting transfers between devices  17.1 us (4%)
  between operations  17 us (4%)
    all_gather x1, waiting for transfers between devices, shards(): weights = lax.all_gather(layer_weight[0], 'dp', axis=1, tiled=True)  146 us
    gather x15, local copies, waits for them, and re-layouts, grouped_product(): chosen = jnp.take(weights, species, axis=0)  97.9 us
    ppermute x6, waiting for transfers between devices, shifted(): return lax.ppermute(block, axis, route)  73.3 us
    psum x1, blocking collectives, shards(): energies = energies.at[finished].set(lax.psum(term, ('section', 'dp')))  45.5 us
    dot_general x7, matrix products, grouped_product(): jnp.einsum('tai,tio->tao', source, chosen, preferred_element_type=jnp.flo...  37.9 us
    ppermute x6, starting transfers between devices, shifted(): return lax.ppermute(block, axis, route)  13.7 us
  transfers between devices with their start and end apart: 8, of which 6 were waited for; matrix products, arithmetic and copies ran while one was open for 20% of the time, Pallas kernels for 0%

commit v1 on v0

--- a/solution.py
+++ b/solution.py
@@ -50,7 +50,7 @@
         first = descriptors[min(step, batches - 1)]
         source = jnp.where(position == 0, first, incoming).reshape(tiles_dev, tile, width)
         if step == 0:
-            weights = lax.all_gather(layer_weight[0], "dp", axis=1, tiled=True)
+            weights = jnp.concatenate(lax.all_gather(layer_weight[0], "dp"), axis=1)
             product = grouped_product(source, weights, species)
         else:
             product = grouped_product(source, weights, species)

time: 466 us -> 466 us (level)
  no operation moved by 1% of the time
where the time goes in v1:
time: 466 us; the launch traced here: 465 us
  waiting for transfers between devices  220 us (47%)
  local copies, waits for them, and re-layouts  102 us (22%)
  blocking collectives  45.5 us (10%)
  matrix products  42.8 us (9%)
  other arithmetic  20.5 us (4%)
  starting transfers between devices  17.1 us (4%)
  between operations  17 us (4%)
    all_gather x1, waiting for transfers between devices, shards(): weights = jnp.concatenate(lax.all_gather(layer_weight[0], 'dp'), axis=1)  146 us
    gather x15, local copies, waits for them, and re-layouts, grouped_product(): chosen = jnp.take(weights, species, axis=0)  97.9 us
    ppermute x6, waiting for transfers between devices, shifted(): return lax.ppermute(block, axis, route)  73.3 us
    psum x1, blocking collectives, shards(): energies = energies.at[finished].set(lax.psum(term, ('section', 'dp')))  45.5 us
    dot_general x7, matrix products, grouped_product(): jnp.einsum('tai,tio->tao', source, chosen, preferred_element_type=jnp.flo...  37.9 us
    ppermute x6, starting transfers between devices, shifted(): return lax.ppermute(block, axis, route)  13.7 us
  transfers between devices with their start and end apart: 8, of which 6 were waited for; matrix products, arithmetic and copies ran while one was open for 20% of the time, Pallas kernels for 0%

profile of v1, /device:TPU:12, one launch (start us, length us, event | category | flops | bytes accessed | tf_op | source)
XLA Modules:
  0.0 464.9 jit_solution(16702947367663745943)
XLA Ops:
  12.9 146.2 %all-gather.2.cloned.1.call-done = bf16[8,8,128,1024]{3,2,0,1:T(8,128)(2,1)} async-done(((bf16[1,8,128,1024]{3,2,0,1:T(8,128)(2,1)}), bf16[8,8,128,1024]{3,2,0,1:T(8,128)(2,1)}) %all-gather.2.cloned.1.call-update) | async-done | bytes 16777232 | tf_op jit(solution)/shard_map/all_gather | solution.py:53
  159.1 11.7 %fusion.131 = (bf16[8,512,1024]{2,1,0:T(8,128)(2,1)}, bf16[8,512,1024]{2,1,0:T(8,128)(2,1)}) fusion(bf16[8,1024,1024]{2,1,0:T(8,128)(2,1)} %bitcast.149), kind=kLoop, calls=%fused_computation.259 | loop fusion | bytes 33554432 | tf_op jit(solution)/shard_map/jit(_take)/gather | solution.py:18
  170.8 6.2 %gather_fusion = bf16[4,512,1024]{2,1,0:T(8,128)(2,1)} fusion(bf16[8,512,1024]{2,1,0:T(8,128)(2,1)} %get-tuple-element.168, s32[1024]{0:T(1024)S(1)} %pad_clamp_fusion.6), kind=kCustom, calls=%fused_computation.clone | custom fusion | bytes 8388624 | tf_op jit(solution)/shard_map/jit(_take)/gather | solution.py:18
  176.9 6.1 %gather_fusion.1 = bf16[4,512,1024]{2,1,0:T(8,128)(2,1)} fusion(bf16[8,512,1024]{2,1,0:T(8,128)(2,1)} %get-tuple-element.169, s32[1024]{0:T(1024)S(1)} %pad_clamp_fusion.6), kind=kCustom, calls=%fused_computation.1.clone | custom fusion | bytes 8388624 | tf_op jit(solution)/shard_map/jit(_take)/gather | solution.py:18
  193.5 6.2 %gather_fusion.2 = bf16[4,512,1024]{2,1,0:T(8,128)(2,1)} fusion(bf16[8,512,1024]{2,1,0:T(8,128)(2,1)} %get-tuple-element.168, s32[1024]{0:T(1024)S(1)} %pad_clamp_fusion.5), kind=kCustom, calls=%fused_computation.2.clone | custom fusion | bytes 8388624 | tf_op jit(solution)/shard_map/jit(_take)/gather | solution.py:18
  199.7 6.1 %gather_fusion.3 = bf16[4,512,1024]{2,1,0:T(8,128)(2,1)} fusion(bf16[8,512,1024]{2,1,0:T(8,128)(2,1)} %get-tuple-element.169, s32[1024]{0:T(1024)S(1)} %pad_clamp_fusion.5), kind=kCustom, calls=%fused_computation.3.clone | custom fusion | bytes 8388624 | tf_op jit(solution)/shard_map/jit(_take)/gather | solution.py:18
  205.8 10.8 %collective-permute-done = bf16[512,1024]{1,0:T(8,128)(2,1)S(1)} collective-permute-done((bf16[512,1024]{1,0:T(8,128)(2,1)S(1)}, bf16[512,1024]{1,0:T(8,128)(2,1)S(1)}, u32[]{:S(2)}, u32[]{:S(2)}) %collective-permute-start) | collective-permute-done | bytes 1048608 | tf_op jit(solution)/shard_map/ppermute | solution.py:10
  217.9 5.4 %fusion.136 = (bf16[4,128,1024]{2,1,0:T(8,128)(2,1)S(1)}, f32[4,128]{1,0:T(4,128)S(1)}) fusion(f32[4,1024]{1,0:T(4,128)S(1)} %fusion.55, f32[4,1024]{1,0:T(4,128)S(1)} %fusion.45, bf16[4,128,1024]{2,1,0:T(8,128)(2,1)S(1)} %bitcast.152, bf16[4,512,1024]{2,1,0:T(8,128)(2,1)} %gather_fusion.3, bf16[4,512,1024]{2,1,0:T(8,128)(2,1)} %gather_fusion.2, ...), kind=kOutput, calls=%fused_computation.264 | convolution fusion | flops 1098907136 | bytes 10520580 | tf_op jit(solution)/shard_map/tai,tio->tao/dot_general | solution.py:19
  227.0 6.2 %gather_fusion.4 = bf16[4,512,1024]{2,1,0:T(8,128)(2,1)} fusion(bf16[8,512,1024]{2,1,0:T(8,128)(2,1)} %get-tuple-element.168, s32[1024]{0:T(1024)S(1)} %pad_clamp_fusion.4), kind=kCustom, calls=%fused_computation.4.clone | custom fusion | bytes 8388624 | tf_op jit(solution)/shard_map/jit(_take)/gather | solution.py:18
  233.2 6.1 %gather_fusion.5 = bf16[4,512,1024]{2,1,0:T(8,128)(2,1)} fusion(bf16[8,512,1024]{2,1,0:T(8,128)(2,1)} %get-tuple-element.169, s32[1024]{0:T(1024)S(1)} %pad_clamp_fusion.4), kind=kCustom, calls=%fused_computation.5.clone | custom fusion | bytes 8388624 | tf_op jit(solution)/shard_map/jit(_take)/gather | solution.py:18
  239.4 11.2 %collective-permute-done.1 = bf16[512,1024]{1,0:T(8,128)(2,1)S(1)} collective-permute-done((bf16[512,1024]{1,0:T(8,128)(2,1)S(1)}, bf16[512,1024]{1,0:T(8,128)(2,1)S(1)}, u32[]{:S(2)}, u32[]{:S(2)}) %collective-permute-start.1) | collective-permute-done | bytes 1048608 | tf_op jit(solution)/shard_map/ppermute | solution.py:10
  260.3 6.2 %gather_fusion.6 = bf16[4,512,1024]{2,1,0:T(8,128)(2,1)} fusion(bf16[8,512,1024]{2,1,0:T(8,128)(2,1)} %get-tuple-element.168, s32[1024]{0:T(1024)S(1)} %pad_clamp_fusion.3), kind=kCustom, calls=%fused_computation.6.clone | custom fusion | bytes 8388624 | tf_op jit(solution)/shard_map/jit(_take)/gather | solution.py:18
  266.5 6.1 %gather_fusion.7 = bf16[4,512,1024]{2,1,0:T(8,128)(2,1)} fusion(bf16[8,512,1024]{2,1,0:T(8,128)(2,1)} %get-tuple-element.169, s32[1024]{0:T(1024)S(1)} %pad_clamp_fusion.3), kind=kCustom, calls=%fused_computation.7.clone | custom fusion | bytes 8388624 | tf_op jit(solution)/shard_map/jit(_take)/gather | solution.py:18
  272.6 11.2 %collective-permute-done.2 = bf16[512,1024]{1,0:T(8,128)(2,1)S(1)} collective-permute-done((bf16[512,1024]{1,0:T(8,128)(2,1)S(1)}, bf16[512,1024]{1,0:T(8,128)(2,1)S(1)}, u32[]{:S(2)}, u32[]{:S(2)}) %collective-permute-start.2) | collective-permute-done | bytes 1048608 | tf_op jit(solution)/shard_map/ppermute | solution.py:10
  285.1 5.4 %fusion.134 = (bf16[4,128,1024]{2,1,0:T(8,128)(2,1)S(1)}, f32[4,128]{1,0:T(4,128)S(1)}) fusion(f32[4,1024]{1,0:T(4,128)S(1)} %fusion.53, f32[4,1024]{1,0:T(4,128)S(1)} %fusion.41, bf16[4,128,1024]{2,1,0:T(8,128)(2,1)S(1)} %bitcast.154, bf16[4,512,1024]{2,1,0:T(8,128)(2,1)} %gather_fusion.7, bf16[4,512,1024]{2,1,0:T(8,128)(2,1)} %gather_fusion.6, ...), kind=kOutput, calls=%fused_computation.262 | convolution fusion | flops 1098907136 | bytes 10520580 | tf_op jit(solution)/shard_map/tai,tio->tao/dot_general | solution.py:19
  293.5 6.3 %gather_fusion.8 = bf16[4,512,1024]{2,1,0:T(8,128)(2,1)} fusion(bf16[8,512,1024]{2,1,0:T(8,128)(2,1)} %get-tuple-element.168, s32[1024]{0:T(1024)S(1)} %pad_clamp_fusion.2), kind=kCustom, calls=%fused_computation.8.clone | custom fusion | bytes 8388624 | tf_op jit(solution)/shard_map/jit(_take)/gather | solution.py:18
  299.8 6.1 %gather_fusion.9 = bf16[4,512,1024]{2,1,0:T(8,128)(2,1)} fusion(bf16[8,512,1024]{2,1,0:T(8,128)(2,1)} %get-tuple-element.169, s32[1024]{0:T(1024)S(1)} %pad_clamp_fusion.2), kind=kCustom, calls=%fused_computation.9.clone | custom fusion | bytes 8388624 | tf_op jit(solution)/shard_map/jit(_take)/gather | solution.py:18
  305.9 6.2 %gather_fusion.10 = bf16[4,512,1024]{2,1,0:T(8,128)(2,1)} fusion(bf16[8,512,1024]{2,1,0:T(8,128)(2,1)} %get-tuple-element.168, s32[1024]{0:T(1024)S(1)} %pad_clamp_fusion.1), kind=kCustom, calls=%fused_computation.10.clone | custom fusion | bytes 8388624 | tf_op jit(solution)/shard_map/jit(_take)/gather | solution.py:18
  312.1 6.2 %gather_fusion.11 = bf16[4,512,1024]{2,1,0:T(8,128)(2,1)} fusion(bf16[8,512,1024]{2,1,0:T(8,128)(2,1)} %get-tuple-element.169, s32[1024]{0:T(1024)S(1)} %pad_clamp_fusion.1), kind=kCustom, calls=%fused_computation.11.clone | custom fusion | bytes 8388624 | tf_op jit(solution)/shard_map/jit(_take)/gather | solution.py:18
  318.2 6.1 %gather_fusion.12 = bf16[4,512,1024]{2,1,0:T(8,128)(2,1)} fusion(bf16[8,512,1024]{2,1,0:T(8,128)(2,1)} %get-tuple-element.168, s32[1024]{0:T(1024)S(1)} %pad_clamp_fusion), kind=kCustom, calls=%fused_computation.12.clone | custom fusion | bytes 8388624 | tf_op jit(solution)/shard_map/jit(_take)/gather | solution.py:18
  324.4 6.2 %gather_fusion.13 = bf16[4,512,1024]{2,1,0:T(8,128)(2,1)} fusion(bf16[8,512,1024]{2,1,0:T(8,128)(2,1)} %get-tuple-element.169, s32[1024]{0:T(1024)S(1)} %pad_clamp_fusion), kind=kCustom, calls=%fused_computation.13.clone | custom fusion | bytes 8388624 | tf_op jit(solution)/shard_map/jit(_take)/gather | solution.py:18
  342.2 21.4 %collective-permute-done.4 = bf16[512,1024]{1,0:T(8,128)(2,1)S(1)} collective-permute-done((bf16[512,1024]{1,0:T(8,128)(2,1)S(1)}, bf16[512,1024]{1,0:T(8,128)(2,1)S(1)}, u32[]{:S(2)}, u32[]{:S(2)}) %collective-permute-start.4) | collective-permute-done | bytes 1048608 | tf_op jit(solution)/shard_map/ppermute | solution.py:10
  376.3 18.7 %collective-permute-done.5 = bf16[512,1024]{1,0:T(8,128)(2,1)S(1)} collective-permute-done((bf16[512,1024]{1,0:T(8,128)(2,1)S(1)}, bf16[512,1024]{1,0:T(8,128)(2,1)S(1)}, u32[]{:S(2)}, u32[]{:S(2)}) %collective-permute-start.5) | collective-permute-done | bytes 1048608 | tf_op jit(solution)/shard_map/ppermute | solution.py:10
  409.5 45.5 %all-reduce.1 = (f32[1]{0:T(128)}, f32[1]{0:T(128)}, f32[1]{0:T(128)}, f32[1]{0:T(128)}) all-reduce(f32[1]{0:T(128)} %bitcast.65, f32[1]{0:T(128)} %bitcast.66, f32[1]{0:T(128)} %bitcast.67, f32[1]{0:T(128)} %bitcast.68), channel_id=1, replica_groups=mesh['section'=4,'dp'=8] {'section','dp'}, use_global_device_ids=true, to_apply=%region_15.17 | all-reduce | flops 4 | bytes 32 | tf_op jit(solution)/shard_map/psum | solution.py:70
  (97 shorter events, 74.2 us)
Async XLA Ops:
  7.2 3.3 copy-start
  7.2 151.9 %all-gather.2.cloned.1.call-start = ((), (), s32[]{:S(2)}) async-start(), calls=%async_computation.1 | async-start | bytes 18874368 | tf_op jit(solution)/shard_map/all_gather | solution.py:53
  183.1 8.8 %copy-start.2 = (s32[2]{0:T(128)S(1)}, s32[2]{0:T(128)}, u32[]{:S(2)}) copy-start(s32[2]{0:T(128)} %constant.301.clone.1) | copy-start | bytes 28
  183.1 9.6 %copy-start.4 = (f32[8]{0:T(128)S(1)}, f32[8]{0:T(128)}, u32[]{:S(2)}) copy-start(f32[8]{0:T(128)} %param.35) | copy-start | bytes 100
  183.1 10.2 %copy-start.3 = (f32[8,1024]{1,0:T(8,128)S(1)}, f32[8,1024]{1,0:T(8,128)}, u32[]{:S(2)}) copy-start(f32[8,1024]{1,0:T(8,128)} %param.34) | copy-start | bytes 98308
  188.5 28.1 %collective-permute-start = (bf16[512,1024]{1,0:T(8,128)(2,1)S(1)}, bf16[512,1024]{1,0:T(8,128)(2,1)S(1)}, u32[]{:S(2)}, u32[]{:S(2)}) collective-permute-start(bf16[512,1024]{1,0:T(8,128)(2,1)S(1)} %bitcast.168), channel_id=1, source_target_pairs={{0,8},{8,16},{16,24},{1,9},{9,17},{17,25},{2,10},{10,18},{18,26},{... | collective-permute-start | bytes 3145736 | tf_op jit(solution)/shard_map/ppermute | solution.py:10
  223.3 27.3 %collective-permute-start.1 = (bf16[512,1024]{1,0:T(8,128)(2,1)S(1)}, bf16[512,1024]{1,0:T(8,128)(2,1)S(1)}, u32[]{:S(2)}, u32[]{:S(2)}) collective-permute-start(bf16[512,1024]{1,0:T(8,128)(2,1)S(1)} %bitcast.170), channel_id=1, source_target_pairs={{0,8},{8,16},{16,24},{1,9},{9,17},{17,25},{2,10},{10,18},{18,26},{... | collective-permute-start | bytes 3145736 | tf_op jit(solution)/shard_map/ppermute | solution.py:10
  257.4 26.4 %collective-permute-start.2 = (bf16[512,1024]{1,0:T(8,128)(2,1)S(1)}, bf16[512,1024]{1,0:T(8,128)(2,1)S(1)}, u32[]{:S(2)}, u32[]{:S(2)}) collective-permute-start(bf16[512,1024]{1,0:T(8,128)(2,1)S(1)} %bitcast.169), channel_id=1, source_target_pairs={{0,8},{8,16},{16,24},{1,9},{9,17},{17,25},{2,10},{10,18},{18,26},{... | collective-permute-start | bytes 3145736 | tf_op jit(solution)/shard_map/ppermute | solution.py:10
  285.1 7.5 %copy-start.1 = (s32[4,4]{1,0:T(4,128)S(1)}, s32[4,4]{1,0:T(4,128)}, u32[]{:S(2)}) copy-start(s32[4,4]{1,0:T(4,128)} %param.37) | copy-start | bytes 196
  290.5 40.7 %collective-permute-start.3 = (bf16[512,1024]{1,0:T(8,128)(2,1)S(1)}, bf16[512,1024]{1,0:T(8,128)(2,1)S(1)}, u32[]{:S(2)}, u32[]{:S(2)}) collective-permute-start(bf16[512,1024]{1,0:T(8,128)(2,1)S(1)} %bitcast.165), channel_id=1, source_target_pairs={{0,8},{8,16},{16,24},{1,9},{9,17},{17,25},{2,10},{10,18},{18,26},{... | collective-permute-start | bytes 3145736 | tf_op jit(solution)/shard_map/ppermute | solution.py:10
  338.0 25.6 %collective-permute-start.4 = (bf16[512,1024]{1,0:T(8,128)(2,1)S(1)}, bf16[512,1024]{1,0:T(8,128)(2,1)S(1)}, u32[]{:S(2)}, u32[]{:S(2)}) collective-permute-start(bf16[512,1024]{1,0:T(8,128)(2,1)S(1)} %bitcast.167), channel_id=1, source_target_pairs={{0,8},{8,16},{16,24},{1,9},{9,17},{17,25},{2,10},{10,18},{18,26},{... | collective-permute-start | bytes 3145736 | tf_op jit(solution)/shard_map/ppermute | solution.py:10
  370.4 24.7 %collective-permute-start.5 = (bf16[512,1024]{1,0:T(8,128)(2,1)S(1)}, bf16[512,1024]{1,0:T(8,128)(2,1)S(1)}, u32[]{:S(2)}, u32[]{:S(2)}) collective-permute-start(bf16[512,1024]{1,0:T(8,128)(2,1)S(1)} %bitcast.166), channel_id=1, source_target_pairs={{0,8},{8,16},{16,24},{1,9},{9,17},{17,25},{2,10},{10,18},{18,26},{... | collective-permute-start | bytes 3145736 | tf_op jit(solution)/shard_map/ppermute | solution.py:10
  403.7 53.8 %all-to-all-start = ((f32[4,1,512]{2,1,0:T(1,128)}), f32[4,1,512]{2,1,0:T(1,128)S(1)}, u32[]{:S(2)}, u32[]{:S(2)}) async-start(f32[4,1,512]{2,1,0:T(1,128)} %constant_dynamic-update-slice_fusion), calls=%async_computation | async-start | bytes 16384 | tf_op jit(solution)/shard_map/all_to_all | solution.py:73
  457.4 0.6 copy-start.5
Sparse Core Ops, SparseCore 0:
  9.6 149.4 all-gather.1
